TPU v7x, 32 devices: a whole 2x2x4 slice. The times are simulated.
32 devices in a mesh: col: 4 (over z), row: 8 (over y, x, core).
Axes of the slice: x: 2, y: 2, z: 4, core: 2. Of those that a mesh axis runs over, the one named last changes fastest.
Arguments:
- queries: bfloat16 [32768, 256], P(('col', 'row')), may hold values from -6 to 6
- keys: bfloat16 [32768, 256], P(('col', 'row')), may hold values from -6 to 6
- values: bfloat16 [32768, 256], P(('col', 'row')), may hold values from -6 to 6
- out_grad: bfloat16 [32768, 256], P(('col', 'row')), may hold values from -6 to 6
- weight_table: float32 [64, 2, 21], replicated, may hold values from 0.25 to 2
- profile: int32 [32768], P(('col', 'row')), may hold values from 0 to 63
Outputs:
- output: float32 [32768, 256], P(('col', 'row'))
- query_grad: float32 [32768, 256], P(('col', 'row'))
- key_grad: float32 [32768, 256], P(('col', 'row'))
- value_grad: float32 [32768, 256], P(('col', 'row'))
All inputs are finite; a program needn't handle non-finite values.
Results may differ from a plain program's by a relative error of at most 0.0034.
Values sent between devices are 32-bit elements; how exact they have to be, the bound alone decides.
A program may use at most 128 MiB of HBM per device.

v0:
```python
import functools
import math

import jax
import jax.numpy as jnp
from jax import lax
from jax.experimental import pallas as pl
from jax.experimental.pallas import tpu as pltpu
from jax.sharding import PartitionSpec as P

MESH = pl.DeviceIdType.MESH
F32 = jnp.float32
BF16 = jnp.bfloat16
NN = (((1,), (0,)), ((), ()))
NT = (((1,), (1,)), ((), ()))
TN = (((0,), (0,)), ((), ()))
CHUNK = 128


def mm(a, b, dims):
    return lax.dot_general(a, b, dims, preferred_element_type=F32)


def main_kernel(
    dims,
    q_hbm, k_hbm, v_hbm, g_hbm, tab_hbm, prof_hbm,
    lo_ref, lq_ref, lk_ref, lv_ref, wq_ref, wg_ref, bnt_ref, bnn_ref, pul_ref, k_ref, v_ref,
    q_ref, g_ref, tab_ref, prof_ref, in_sem,
    w_scr, lev_scr, m_scr, p_scr, d_scr,
    st, x0, pin, sum1, ain, b1, b2, tot, zout, zin, far,
    pair_send, pair_recv, red_send, red_recv, low_send, low_recv, z_send, z_recv, ga_send, ga_recv, gb_send, gb_recv,
):
    T, H, D, cols, rows, span = dims
    rows_bits = rows.bit_length() - 1
    col_bits = cols.bit_length() - 1
    L = rows_bits + col_bits
    chips = rows // 2
    qb = rows_bits - 1
    R = D // chips
    tile_bits = T.bit_length() - 1
    span_bits = span.bit_length() - 1
    z = lax.axis_index("col")
    row = lax.axis_index("row")
    core = lax.rem(row, 2)
    chip = lax.div(row, 2)
    other = 1 - core

    def chip_at(offset):
        return lax.rem(chip + offset, chips)

    def col_at(offset):
        return lax.rem(z + offset, cols)

    loads = [
        pltpu.make_async_copy(src, dst, in_sem.at[n])
        for n, (src, dst) in enumerate(
            [(prof_hbm, prof_ref), (tab_hbm, tab_ref), (q_hbm, q_ref), (g_hbm, g_ref),
             (v_hbm, v_ref), (k_hbm, k_ref)]
        )
    ]
    for load in loads:
        load.start()
    barrier = pltpu.get_barrier_semaphore()
    pl.semaphore_signal(barrier, inc=1, device_id=(z, chip * 2 + other), device_id_type=MESH)
    for offset in range(1, chips):
        pl.semaphore_signal(
            barrier, inc=1, device_id=(z, chip_at(offset) * 2 + core), device_id_type=MESH
        )
    for offset in range(1, cols):
        pl.semaphore_signal(barrier, inc=1, device_id=(col_at(offset), row), device_id_type=MESH)

    def remote(src, dst, send, recv, device):
        return pltpu.make_async_remote_copy(
            src_ref=src, dst_ref=dst, send_sem=send, recv_sem=recv,
            device_id=device, device_id_type=MESH,
        )

    profiles = tab_ref.shape[0]
    levels = tab_ref.shape[2]
    loads[0].wait()
    loads[1].wait()
    onehot = jnp.where(
        lax.broadcasted_iota(jnp.int32, (profiles, T), 0) == prof_ref[...], 1.0, 0.0
    ).astype(BF16)
    onehot = jnp.concatenate([onehot, onehot, onehot], axis=0)
    place = lax.broadcasted_iota(jnp.int32, (profiles, levels), 1)
    scale = jnp.zeros((profiles, levels), F32)
    for level in range(levels):
        scale = jnp.where(place == level, 2.0 ** (-0.5 * level) / math.sqrt(D), scale)
    for h in range(H):
        table = tab_ref[:, h, :] * scale
        top = table.astype(BF16)
        rest = table - top.astype(F32)
        mid = rest.astype(BF16)
        low = (rest - mid.astype(F32)).astype(BF16)
        w_scr[h] = mm(onehot, jnp.concatenate([top, mid, low], axis=0), TN)

    def weigh(src, dst, h):
        for start in range(0, T, CHUNK):
            rs = slice(start, start + CHUNK)
            x = src[rs, h * D : (h + 1) * D].astype(F32)
            for j in range(L):
                level = tile_bits + 1 + j
                c = (h * L + j) * D
                dst[rs, c : c + D] = (x * w_scr[h, rs, level : level + 1]).astype(BF16)

    high = 1 + col_bits
    slot = [0] + [high + j for j in range(qb)] + [1 + jj for jj in range(col_bits)]
    for load in loads[2:]:
        load.wait()
    for h in range(H):
        hs = slice(h * D, (h + 1) * D)
        weigh(q_ref, wq_ref, h)
        state = mm(v_ref[:, hs], k_ref[:, hs], TN)
        grads = mm(g_ref[:, hs], wq_ref[:, h * L * D : (h + 1) * L * D], TN)
        st[h, 0] = state
        for j in range(1, L):
            st[h, slot[j]] = grads[:, j * D : (j + 1) * D]
        x0[h] = jnp.where(core == 0, state, grads[:, :D])

    pl.semaphore_wait(barrier, chips + cols - 1)
    partner = (z, chip * 2 + other)
    pair = remote(st.at[other], pin, pair_send.at[0], pair_recv.at[0], partner)
    pair.start()
    near = remote(x0, far.at[0], pair_send.at[1], pair_recv.at[1], partner)
    near.start()

    r_at = lax.broadcasted_iota(jnp.int32, (span, span), 0)
    c_at = lax.broadcasted_iota(jnp.int32, (span, span), 1)
    apart = jnp.bitwise_xor(r_at, c_at)
    lev = jnp.zeros((span, span), jnp.int32)
    for bit in range(span_bits):
        lev = lev + jnp.where(apart >= 1 << bit, 1, 0)
    lev_scr[...] = jnp.where(c_at <= r_at, lev, -1)

    last = T // span - 1

    def unit(h, i):
        hs = slice(h * D, (h + 1) * D)
        ts = slice(i * span, (i + 1) * span)
        width = (i + 1) * span
        for start in range(0, span, 64):
            rs = slice(start, start + 64)
            wts = slice(i * span + start, i * span + start + 64)
            mask = jnp.zeros((64, span), F32)
            here = lev_scr[rs, :]
            for level in range(span_bits + 1):
                mask = jnp.where(here == level, w_scr[h, wts, level : level + 1], mask)
            m_scr[rs, :] = mask
        q = q_ref[ts, hs]
        g = g_ref[ts, hs]
        for b in range(i + 1):
            bs = slice(b * span, (b + 1) * span)
            if b < i:
                level = span_bits + (b ^ i).bit_length()
                mask = w_scr[h, ts, level : level + 1]
            else:
                mask = m_scr[...]
            p_scr[:, bs] = (mm(q, k_ref[bs, hs], NT) * mask).astype(BF16)
            d_scr[:, bs] = (mm(g, v_ref[bs, hs], NT) * mask).astype(BF16)
        ws = slice(0, width)
        lo_ref[ts, hs] = mm(p_scr[:, ws], v_ref[ws, hs], NN)
        lq_ref[ts, hs] = mm(d_scr[:, ws], k_ref[ws, hs], NN)
        dk = mm(d_scr[:, ws], q, TN)
        dv = mm(p_scr[:, ws], g, TN)
        if i == last:
            lk_ref[ws, hs] = dk
            lv_ref[ws, hs] = dv
        else:
            lk_ref[ws, hs] += dk
            lv_ref[ws, hs] += dv

    work = [(h, i) for i in range(last, -1, -1) for h in range(H)]
    cut1 = 1
    cut2 = max(cut1, len(work) * 4 // 8)
    cut3 = max(cut2, len(work) * 6 // 8)

    for h, i in work[:cut1]:
        unit(h, i)

    pair.wait()
    for p in range(chips):
        rs = slice(p * R, (p + 1) * R)
        sum1[p] = st[core, :, rs, :] + pin[:, rs, :]
    reduces = []
    lows = []
    for offset in range(1, chips):
        to = chip_at(offset)
        copy = remote(
            sum1.at[to, pl.ds(0, high)], ain.at[chip, pl.ds(0, high)],
            red_send.at[offset], red_recv.at[offset], (z, to * 2 + core),
        )
        copy.start()
        reduces.append(copy)
    if qb:
        for offset in range(1, chips):
            to = chip_at(offset)
            copy = remote(
                sum1.at[to, pl.ds(high, qb)], ain.at[chip, pl.ds(high, qb)],
                low_send.at[offset], low_recv.at[offset], (z, to * 2 + core),
            )
            copy.start()
            lows.append(copy)
    ain[chip] = sum1[chip]

    for h, i in work[cut1:cut2]:
        unit(h, i)

    for copy in reduces:
        copy.wait()
    tot[0] = sum([ain[p, 0] for p in range(1, chips)], ain[0, 0])
    for jj in range(col_bits):
        tot[1 + jj] = sum([ain[p, 1 + jj] for p in range(1, chips)], ain[0, 1 + jj])

    def sibling(mine, theirs, bit):
        same = lax.div(mine, 2 << bit) == theirs >> bit + 1
        differs = lax.rem(lax.div(mine, 1 << bit), 2) != theirs >> bit & 1
        return jnp.logical_and(same, differs)

    for to in range(cols):
        value = jnp.zeros((R, D), F32)
        for jj in range(col_bits):
            piece = tot[0] if to >> jj & 1 else tot[1 + jj]
            value = jnp.where(sibling(z, to, jj), piece, value)
        zout[to] = value
    crosses = []
    for offset in range(1, cols):
        to = col_at(offset)
        copy = remote(
            zout.at[to], zin.at[z], z_send.at[offset], z_recv.at[offset], (to, row)
        )
        copy.start()
        crosses.append(copy)
    zin[z] = jnp.zeros((R, D), F32)

    mine = pl.ds(pl.multiple_of(chip * R, R), R)
    firsts = []
    if qb:
        for copy in lows:
            copy.wait()
        for to in range(chips):
            for jj in range(qb):
                source = 0 if to >> jj & 1 else high + jj
                group = [
                    p for p in range(chips)
                    if p >> jj + 1 == to >> jj + 1 and (p >> jj & 1) != (to >> jj & 1)
                ]
                b1[to, jj] = sum([ain[p, source] for p in group[1:]], ain[group[0], source])
        for offset in range(1, chips):
            to = chip_at(offset)
            copy = remote(
                b1.at[to], far.at[pl.ds(1, qb), core, mine], ga_send.at[offset],
                ga_recv.at[offset], (z, to * 2 + core),
            )
            copy.start()
            firsts.append(copy)
        for jj in range(qb):
            far[1 + jj, core, mine] = b1[chip, jj]

    for h, i in work[cut2:cut3]:
        unit(h, i)

    for copy in crosses:
        copy.wait()
    for jj in range(col_bits):
        value = jnp.zeros((R, D), F32)
        for source in range(cols):
            value = value + jnp.where(sibling(z, source, jj), zin[source], 0.0)
        b2[jj] = value
    seconds = []
    if col_bits:
        for offset in range(1, chips):
            to = chip_at(offset)
            copy = remote(
                b2, far.at[pl.ds(1 + qb, col_bits), core, mine], gb_send.at[offset],
                gb_recv.at[offset], (z, to * 2 + core),
            )
            copy.start()
            seconds.append(copy)
        for jj in range(col_bits):
            far[1 + qb + jj, core, mine] = b2[jj]
    relays = []
    if qb:
        for copy in firsts:
            copy.wait()
        relay = remote(
            far.at[pl.ds(1, qb), core], far.at[pl.ds(1, qb), core],
            pair_send.at[2], pair_recv.at[2], partner,
        )
        relay.start()
        relays.append(relay)

    for h, i in work[cut3:]:
        unit(h, i)
    for h in range(H):
        weigh(g_ref, wg_ref, h)

    if col_bits:
        for copy in seconds:
            copy.wait()
        relay = remote(
            far.at[pl.ds(1 + qb, col_bits), core], far.at[pl.ds(1 + qb, col_bits), core],
            pair_send.at[3], pair_recv.at[3], partner,
        )
        relay.start()
        relays.append(relay)
    near.wait()
    for relay in relays:
        relay.wait()

    digits = [core]
    digits += [lax.rem(lax.div(chip, 1 << jj), 2) for jj in range(qb)]
    digits += [lax.rem(lax.div(z, 1 << jj), 2) for jj in range(col_bits)]
    for h in range(H):
        pulled = jnp.zeros((D, D), F32)
        for j in range(L):
            value = far[j, h]
            up = digits[j] == 1
            pulled = pulled + jnp.where(up, 0.0, value)
            half = jnp.where(up, value, 0.0).astype(BF16)
            bnt_ref[h, :, j * D : (j + 1) * D] = half
            bnn_ref[h, j * D : (j + 1) * D, :] = half
        pul_ref[h] = pulled.astype(BF16)


def finish_kernel(
    dims, lo, lq, lk, lv, wq, wg, k, v, bnt, bnn, pul, out, dq, dk, dv
):
    H, D, L, block = dims
    ts = pl.ds(pl.multiple_of(pl.program_id(0) * block, block), block)
    for h in range(H):
        hs = slice(h * D, (h + 1) * D)
        ls = slice(h * L * D, (h + 1) * L * D)
        out[:, hs] = lo[ts, hs] + mm(wq[ts, ls], bnt[h], NT)
        dq[:, hs] = lq[ts, hs] + mm(wg[ts, ls], bnn[h], NN)
        dk[:, hs] = lk[ts, hs] + mm(v[ts, hs], pul[h], NN)
        dv[:, hs] = lv[ts, hs] + mm(k[ts, hs], pul[h], NT)


def shards(cols, rows, queries, keys, values, out_grad, weight_table, profile):
    T = queries.shape[0]
    H = weight_table.shape[1]
    D = queries.shape[1] // H
    levels = weight_table.shape[2]
    L = rows.bit_length() + cols.bit_length() - 2
    chips = rows // 2
    qb = rows.bit_length() - 2
    col_bits = cols.bit_length() - 1
    R = D // chips
    span = min(T, 256)
    assert H == 2 and R % 8 == 0
    vm = pl.BlockSpec(memory_space=pltpu.VMEM)
    sds = jax.ShapeDtypeStruct
    dma = pltpu.SemaphoreType.DMA
    local = sds((T, H * D), F32)
    weighted = sds((T, H * L * D), BF16)
    parts = pl.pallas_call(
        functools.partial(main_kernel, (T, H, D, cols, rows, span)),
        out_shape=[
            local, local, local, local, weighted, weighted,
            sds((H, D, L * D), BF16), sds((H, L * D, D), BF16), sds((H, D, D), BF16),
            sds((T, H * D), BF16), sds((T, H * D), BF16),
        ],
        in_specs=[pl.BlockSpec(memory_space=pltpu.HBM)] * 6,
        out_specs=[vm] * 11,
        scratch_shapes=[
            pltpu.VMEM((T, H * D), BF16),
            pltpu.VMEM((T, H * D), BF16),
            pltpu.VMEM(weight_table.shape, F32),
            pltpu.VMEM((1, T), jnp.int32),
            dma((6,)),
            pltpu.VMEM((H, T, levels), F32),
            pltpu.VMEM((span, span), jnp.int32),
            pltpu.VMEM((span, span), F32),
            pltpu.VMEM((span, T), BF16),
            pltpu.VMEM((span, T), BF16),
            pltpu.VMEM((H, L, D, D), F32),
            pltpu.VMEM((H, D, D), F32),
            pltpu.VMEM((L, D, D), F32),
            pltpu.VMEM((chips, L, R, D), F32),
            pltpu.VMEM((chips, L, R, D), F32),
            pltpu.VMEM((chips, max(qb, 1), R, D), F32),
            pltpu.VMEM((max(col_bits, 1), R, D), F32),
            pltpu.VMEM((1 + col_bits, R, D), F32),
            pltpu.VMEM((cols, R, D), F32),
            pltpu.VMEM((cols, R, D), F32),
            pltpu.VMEM((L, H, D, D), F32),
            dma((4,)), dma((4,)),
            dma((chips,)), dma((chips,)),
            dma((chips,)), dma((chips,)),
            dma((cols,)), dma((cols,)),
            dma((chips,)), dma((chips,)),
            dma((chips,)), dma((chips,)),
        ],
        compiler_params=pltpu.CompilerParams(
            collective_id=0, has_side_effects=True, vmem_limit_bytes=40 * 1024 * 1024
        ),
        name="main",
    )(*[pltpu.with_memory_space_constraint(a, pltpu.HBM) for a in (queries, keys, values, out_grad, weight_table, profile.reshape(1, T))])
    lo, lq, lk, lv, wq, wg, bnt, bnn, pul, k_near, v_near = parts
    block = min(T, 256)
    tile = pl.BlockSpec((block, H * D), lambda i: (i, 0))
    return pl.pallas_call(
        functools.partial(finish_kernel, (H, D, L, block)),
        grid=(T // block,),
        out_shape=[local] * 4,
        in_specs=[vm] * 11,
        out_specs=[tile] * 4,
        compiler_params=pltpu.CompilerParams(vmem_limit_bytes=24 * 1024 * 1024),
        name="finish",
    )(lo, lq, lk, lv, wq, wg, k_near, v_near, bnt, bnn, pul)


def solution(mesh):
    tokens = P(("col", "row"), None)
    return jax.shard_map(
        functools.partial(shards, mesh.shape["col"], mesh.shape["row"]),
        mesh=mesh,
        in_specs=(tokens,) * 4 + (P(), P(("col", "row"))),
        out_specs=(tokens,) * 4,
        check_vma=False,
    )
```

profile of v0, /device:TPU:0, one launch (start us, length us, event | category | flops | bytes accessed | tf_op | source)
XLA Modules:
  0.0 28.1 jit_solution(13889160884159090450)
XLA Ops:
  0.6 1.5 %copy.10.tab_hbm = f32[64,2,21]{2,1,0:T(2,128)} copy(f32[64,2,21]{0,1,2:T(2,128)} %param.10) | data formatting | bytes 21504 | tf_op args[4]
  2.1 22.4 %main.1 = (f32[1024,256]{1,0:T(8,128)S(1)}, f32[1024,256]{1,0:T(8,128)S(1)}, f32[1024,256]{1,0:T(8,128)S(1)}, f32[1024,256]{1,0:T(8,128)S(1)}, bf16[1024,1280]{1...) custom-call(bf16[1024,256]{1,0:T(8,128)(2,1)} %q_hbm.1, ...), custom_call_target="tpu_custom_call" | custom-call | tf_op jit(solution)/shard_map/main/pallas_call | solution.py:357
  24.5 3.6 %finish.1 = (f32[1024,256]{1,0:T(8,128)}, f32[1024,256]{1,0:T(8,128)}, f32[1024,256]{1,0:T(8,128)}, f32[1024,256]{1,0:T(8,128)}) custom-call(f32[1024,256]{1,0:T(8,128)S(1)} %get-tuple-element.15.lo, f32[1024,256]{1,0:T(8,128)S(1)} %get-tuple-element.16.lq, f32[1024,256]{1,0:T(8,128)S(1)} %get-tuple-element.17.lk, f32[1024,256]{1,0:T(8,128)S(1)} %get-tuple-element.18.lv, ...), custom_call_target="tpu_custom_call" | custom-call | tf_op jit(solution)/shard_map/finish/pallas_call | solution.py:403
where the time goes:
time: 28.3 us; the launch traced here: 28.1 us
  Pallas kernels  26 us (92%)
  local copies, waits for them, and re-layouts  1.45 us (5%)
  between operations  0.64 us (2%)
    pallas_call x1, Pallas kernels, shards(): pl.pallas_call(functools.partial(main_kernel, (T, H, D, cols, rows, span)...  22.4 us
    pallas_call x1, Pallas kernels, shards(): pl.pallas_call(functools.partial(finish_kernel, (H, D, L, block)), grid=(...  3.58 us
    unnamed x1, local copies, waits for them, and re-layouts  1.45 us

commit v1 on v0

v1 whole, which is shorter than its diff:
```python
import functools
import math

import jax
import jax.numpy as jnp
from jax import lax
from jax.experimental import pallas as pl
from jax.experimental.pallas import tpu as pltpu
from jax.sharding import PartitionSpec as P

MESH = pl.DeviceIdType.MESH
F32 = jnp.float32
BF16 = jnp.bfloat16
NN = (((1,), (0,)), ((), ()))
NT = (((1,), (1,)), ((), ()))
TN = (((0,), (0,)), ((), ()))
CHUNK = 128
WIDE = 64
CUTS = (1, 2, 3, 6)


def mm(a, b, dims):
    return lax.dot_general(a, b, dims, preferred_element_type=F32)


def main_kernel(
    dims,
    q_hbm, k_hbm, v_hbm, g_hbm, tab_hbm, prof_hbm,
    lo_ref, lq_ref, lk_ref, lv_ref, wq_ref, wg_ref, bnt_ref, bnn_ref, pul_ref, k_ref, v_ref,
    q_ref, g_ref, tab_ref, prof_ref, in_sem,
    tbl_scr, w_scr, lev_scr, m_scr, p_scr, d_scr,
    s_scr, st, x0, pin, tots, far, ains, outs,
    pair_send, pair_recv, a_send, a_recv, b_send, b_recv, c_send, c_recv,
):
    T, H, D, cols, rows, span = dims
    chip_bits = rows.bit_length() - 2
    bits = chip_bits + cols.bit_length() - 1
    L = bits + 1
    top = L - 1
    tile_bits = T.bit_length() - 1
    span_bits = span.bit_length() - 1
    z = lax.axis_index("col")
    row = lax.axis_index("row")
    core = lax.rem(row, 2)
    chip = lax.div(row, 2)
    other = 1 - core
    digits = [lax.rem(lax.div(chip, 1 << i), 2) for i in range(chip_bits)]
    digits += [lax.rem(lax.div(z, 1 << i), 2) for i in range(bits - chip_bits)]
    upper = [core] + digits

    def flipped(flip, low, high):
        total = 0
        for i in range(low, high):
            digit = 1 - digits[i] if flip >> i & 1 else digits[i]
            total = total + digit * (1 << i - low)
        return total

    def device(flip, which):
        return (flipped(flip, chip_bits, bits), flipped(flip, 0, chip_bits) * 2 + which)

    loads = [
        pltpu.make_async_copy(src, dst, in_sem.at[n])
        for n, (src, dst) in enumerate(
            [(prof_hbm, prof_ref), (tab_hbm, tab_ref), (q_hbm, q_ref), (g_hbm, g_ref),
             (v_hbm, v_ref), (k_hbm, k_ref)]
        )
    ]
    for load in loads:
        load.start()
    half = 1 << top - 1
    barrier = pltpu.get_barrier_semaphore()
    greeted = [(flip, which) for flip in range(half) for which in (core, other)][1:]
    greeted.append((half, core))
    for flip, which in greeted:
        pl.semaphore_signal(barrier, inc=1, device_id=device(flip, which), device_id_type=MESH)

    def remote(src, dst, send, recv, to):
        return pltpu.make_async_remote_copy(
            src_ref=src, dst_ref=dst, send_sem=send, recv_sem=recv,
            device_id=to, device_id_type=MESH,
        )

    profiles = tab_ref.shape[2]
    levels = tab_ref.shape[0]
    tbl_scr[...] = jnp.zeros_like(tbl_scr)
    loads[0].wait()
    loads[1].wait()
    onehot = jnp.where(
        lax.broadcasted_iota(jnp.int32, (profiles, T), 0) == prof_ref[...], 1.0, 0.0
    ).astype(BF16)
    onehot = jnp.concatenate([onehot, onehot, onehot], axis=0)
    place = lax.broadcasted_iota(jnp.int32, (levels, profiles), 0)
    scale = jnp.zeros((levels, profiles), F32)
    for level in range(levels):
        scale = jnp.where(place == level, 2.0 ** (-0.5 * level) / math.sqrt(D), scale)
    for h in range(H):
        tbl_scr[:, h * WIDE : h * WIDE + levels] = jnp.transpose(tab_ref[:, h, :] * scale)
    table = tbl_scr[...]
    first = table.astype(BF16)
    rest = table - first.astype(F32)
    second = rest.astype(BF16)
    third = (rest - second.astype(F32)).astype(BF16)
    w_scr[...] = mm(onehot, jnp.concatenate([first, second, third], axis=0), TN)

    def column(h, rs, level):
        at = h * WIDE + level
        return w_scr[rs, at : at + 1]

    def weigh(src, dst, h, js):
        for start in range(0, T, CHUNK):
            rs = slice(start, start + CHUNK)
            x = src[rs, h * D : (h + 1) * D].astype(F32)
            for j in js:
                c = (h * L + j) * D
                dst[rs, c : c + D] = (x * column(h, rs, tile_bits + 1 + j)).astype(BF16)

    def heads(h):
        return slice(h * D, (h + 1) * D)

    loads[2].wait()
    for h in range(H):
        weigh(q_ref, wq_ref, h, [top])
    loads[3].wait()
    grads = [
        mm(g_ref[:, heads(h)], wq_ref[:, (h * L + top) * D : (h * L + L) * D], TN) for h in range(H)
    ]
    loads[4].wait()
    loads[5].wait()
    for h in range(H):
        s_scr[h] = mm(v_ref[:, heads(h)], k_ref[:, heads(h)], TN)
        st[top, h] = jnp.where(upper[top] == 1, grads[h], s_scr[h])

    def size(j):
        owners = min(1 << j - 1, D // 8)
        return 1 << j - 1, owners, D // owners

    def piece(index, R):
        return pl.ds(pl.multiple_of(index * R, R), R)

    direct = half <= D // 8

    def start_direct():
        n, owners, R = size(top)
        mine = flipped(0, 0, top - 1)
        for flip in range(n - 1, -1, -1):
            owner = flipped(flip, 0, top - 1)
            for which in (core, other):
                if flip == 0 and which is core:
                    continue
                remote(
                    st.at[top, which, piece(owner, R)], ains[top].at[mine * 2 + core],
                    a_send.at[top], a_recv.at[top], device(flip, which),
                ).start()
        ains[top][mine * 2 + core] = st[top, core, piece(mine, R), :]

    def start_reduce(j, source):
        n, owners, R = size(j)
        mine = flipped(0, 0, j - 1)
        for flip in range(n - 1, 0, -1):
            owner = flipped(flip, 0, j - 1)

            def send():
                remote(
                    source.at[piece(owner, R)], ains[j].at[mine],
                    a_send.at[j], a_recv.at[j], device(flip, core),
                ).start()

            if owners < n:
                pl.when(owner < owners)(send)
            else:
                send()
        if owners < n:
            @pl.when(mine < owners)
            def _():
                ains[j][mine] = source[piece(mine, R), :]
        else:
            ains[j][mine] = source[piece(mine, R), :]

    def spread(j):
        n, owners, R = size(j)
        mine = flipped(0, 0, j - 1)
        count = ains[j].shape[0]

        def go():
            if count > 1:
                got = ains[j].at[pl.ds(0, count - 1)]
                remote(got, got, a_send.at[j], a_recv.at[j], device(half, core)).wait_recv()
            outs[j][...] = sum([ains[j][p] for p in range(1, count)], ains[j][0])
            for flip in range(n, 2 * n):
                remote(
                    outs[j], far.at[j, core, piece(mine, R)],
                    b_send.at[j], b_recv.at[j], device(flip, core),
                ).start()

        if owners < n:
            pl.when(mine < owners)(go)
        else:
            go()

    def arrived(j):
        whole = far.at[j, core]
        remote(whole, whole, b_send.at[j], b_recv.at[j], device(half, core)).wait_recv()

    def settle(j):
        n, owners, R = size(j)
        mine = flipped(0, 0, j - 1)
        count = ains[j].shape[0]

        def sent(ref, sem):
            remote(ref, ref, sem, a_recv.at[j], device(half, core)).wait_send()

        if owners < n:
            for flip in range(n - 1, 0, -1):
                @pl.when(flipped(flip, 0, j - 1) < owners)
                def _():
                    sent(outs[j], a_send.at[j])

            @pl.when(mine < owners)
            def _():
                sent(ains[j], b_send.at[j])
        else:
            if count > 1:
                sent(ains[j].at[pl.ds(0, count - 1)], a_send.at[j])
            sent(ains[j].at[pl.ds(0, n)], b_send.at[j])

    pl.semaphore_wait(barrier, len(greeted))
    if direct:
        start_direct()
    for h in range(H):
        weigh(q_ref, wq_ref, h, range(top))
        low = mm(g_ref[:, heads(h)], wq_ref[:, h * L * D : (h * L + top) * D], TN)
        state = s_scr[h]
        for j in range(1, top):
            st[j, h] = jnp.where(upper[j] == 1, low[:, j * D : (j + 1) * D], state)
        x0[h] = jnp.where(core == 0, state, low[:, :D])
    partner = device(0, other)
    pooled = top if direct else L
    pair = remote(
        st.at[pl.ds(1, pooled - 1), other], pin, pair_send.at[0], pair_recv.at[0], partner
    )
    pair.start()
    near = remote(x0, far.at[0], pair_send.at[1], pair_recv.at[1], partner)
    near.start()

    r_at = lax.broadcasted_iota(jnp.int32, (span, span), 0)
    c_at = lax.broadcasted_iota(jnp.int32, (span, span), 1)
    apart = jnp.bitwise_xor(r_at, c_at)
    lev = jnp.zeros((span, span), jnp.int32)
    for bit in range(span_bits):
        lev = lev + jnp.where(apart >= 1 << bit, 1, 0)
    lev_scr[...] = jnp.where(c_at <= r_at, lev, -1)

    last = T // span - 1

    def unit(h, i):
        hs = heads(h)
        ts = slice(i * span, (i + 1) * span)
        width = (i + 1) * span
        for start in range(0, span, 64):
            rs = slice(start, start + 64)
            wts = slice(i * span + start, i * span + start + 64)
            mask = jnp.zeros((64, span), F32)
            here = lev_scr[rs, :]
            for level in range(span_bits + 1):
                mask = jnp.where(here == level, column(h, wts, level), mask)
            m_scr[rs, :] = mask
        q = q_ref[ts, hs]
        g = g_ref[ts, hs]
        for b in range(i + 1):
            bs = slice(b * span, (b + 1) * span)
            if b < i:
                mask = column(h, ts, span_bits + (b ^ i).bit_length())
            else:
                mask = m_scr[...]
            p_scr[:, bs] = (mm(q, k_ref[bs, hs], NT) * mask).astype(BF16)
            d_scr[:, bs] = (mm(g, v_ref[bs, hs], NT) * mask).astype(BF16)
        ws = slice(0, width)
        lo_ref[ts, hs] = mm(p_scr[:, ws], v_ref[ws, hs], NN)
        lq_ref[ts, hs] = mm(d_scr[:, ws], k_ref[ws, hs], NN)
        dk = mm(d_scr[:, ws], q, TN)
        dv = mm(p_scr[:, ws], g, TN)
        if i == last:
            lk_ref[ws, hs] = dk
            lv_ref[ws, hs] = dv
        else:
            lk_ref[ws, hs] += dk
            lv_ref[ws, hs] += dv

    work = [(h, i) for i in range(last, -1, -1) for h in range(H)]

    def units(start, end):
        for h, i in work[len(work) * start // 8 : len(work) * end // 8]:
            unit(h, i)

    units(0, CUTS[0])
    pair.wait()
    for j in range(pooled - 1, 0, -1):
        tots[j - 1] = st[j, core] + pin[j - 1]
        if j == 1:
            ains[1][0] = tots[0]
        else:
            start_reduce(j, tots.at[j - 1])
    spread(1)
    units(CUTS[0], CUTS[1])
    spread(top)
    units(CUTS[1], CUTS[2])
    for j in range(top - 1, 1, -1):
        spread(j)
    units(CUTS[2], CUTS[3])
    for h in range(H):
        weigh(g_ref, wg_ref, h, range(L))

    def relay(low, high, n):
        ref = far.at[pl.ds(low, high - low), core]
        copy = remote(ref, ref, c_send.at[n], c_recv.at[n], partner)
        copy.start()
        return copy

    for j in range(1, top):
        arrived(j)
    early = relay(1, top, 0)
    units(CUTS[3], 8)
    near.wait()
    early.wait_recv()

    def gather(h, js, pulled):
        for j in js:
            value = far[j, h]
            up = upper[j] == 1
            pulled = pulled + jnp.where(up, 0.0, value)
            chosen = jnp.where(up, value, 0.0).astype(BF16)
            bnt_ref[h, :, j * D : (j + 1) * D] = chosen
            bnn_ref[h, j * D : (j + 1) * D, :] = chosen
        return pulled

    for h in range(H):
        s_scr[h] = gather(h, range(top), jnp.zeros((D, D), F32))
    arrived(top)
    late = relay(top, L, 1)
    for j in range(1, L):
        settle(j)
    early.wait_send()
    late.wait()
    for h in range(H):
        pul_ref[h] = gather(h, [top], s_scr[h]).astype(BF16)


def finish_kernel(
    dims, lo, lq, lk, lv, wq, wg, k, v, bnt, bnn, pul, out, dq, dk, dv
):
    H, D, L, block = dims
    ts = pl.ds(pl.multiple_of(pl.program_id(0) * block, block), block)
    for h in range(H):
        hs = slice(h * D, (h + 1) * D)
        ls = slice(h * L * D, (h + 1) * L * D)
        out[:, hs] = lo[ts, hs] + mm(wq[ts, ls], bnt[h], NT)
        dq[:, hs] = lq[ts, hs] + mm(wg[ts, ls], bnn[h], NN)
        dk[:, hs] = lk[ts, hs] + mm(v[ts, hs], pul[h], NN)
        dv[:, hs] = lv[ts, hs] + mm(k[ts, hs], pul[h], NT)


def shards(cols, rows, queries, keys, values, out_grad, weight_table, profile):
    T = queries.shape[0]
    H = weight_table.shape[1]
    D = queries.shape[1] // H
    levels = weight_table.shape[2]
    L = rows.bit_length() + cols.bit_length() - 2
    profiles = weight_table.shape[0]
    top = L - 1
    direct = 1 << top - 1 <= D // 8
    span = min(T, 256)
    assert H == 2 and L > 2 and H * WIDE == 128 and levels <= WIDE
    pieces = [(8, D), (1, D, D)]
    for j in range(2, L):
        n = 1 << j - 1
        R = D // min(n, D // 8)
        pieces.append((n * (2 if direct and j == top else 1), R, D))
    vm = pl.BlockSpec(memory_space=pltpu.VMEM)
    sds = jax.ShapeDtypeStruct
    dma = pltpu.SemaphoreType.DMA
    local = sds((T, H * D), F32)
    weighted = sds((T, H * L * D), BF16)
    parts = pl.pallas_call(
        functools.partial(main_kernel, (T, H, D, cols, rows, span)),
        out_shape=[
            local, local, local, local, weighted, weighted,
            sds((H, D, L * D), BF16), sds((H, L * D, D), BF16), sds((H, D, D), BF16),
            sds((T, H * D), BF16), sds((T, H * D), BF16),
        ],
        in_specs=[pl.BlockSpec(memory_space=pltpu.HBM)] * 6,
        out_specs=[vm] * 11,
        scratch_shapes=[
            pltpu.VMEM((T, H * D), BF16),
            pltpu.VMEM((T, H * D), BF16),
            pltpu.VMEM((levels, H, profiles), F32),
            pltpu.VMEM((1, T), jnp.int32),
            dma((6,)),
            pltpu.VMEM((profiles, H * WIDE), F32),
            pltpu.VMEM((T, H * WIDE), F32),
            pltpu.VMEM((span, span), jnp.int32),
            pltpu.VMEM((span, span), F32),
            pltpu.VMEM((span, T), BF16),
            pltpu.VMEM((span, T), BF16),
            pltpu.VMEM((H, D, D), F32),
            pltpu.VMEM((L, H, D, D), F32),
            pltpu.VMEM((H, D, D), F32),
            pltpu.VMEM(((top if direct else L) - 1, D, D), F32),
            pltpu.VMEM(((top if direct else L) - 1, D, D), F32),
            pltpu.VMEM((L, H, D, D), F32),
            [pltpu.VMEM(shape, F32) for shape in pieces],
            [pltpu.VMEM(shape[-2:], F32) for shape in pieces],
            dma((2,)), dma((2,)),
            dma((L,)), dma((L,)),
            dma((L,)), dma((L,)),
            dma((2,)), dma((2,)),
        ],
        compiler_params=pltpu.CompilerParams(
            collective_id=0, has_side_effects=True, vmem_limit_bytes=40 * 1024 * 1024
        ),
        name="main",
    )(*[pltpu.with_memory_space_constraint(a, pltpu.HBM) for a in (queries, keys, values, out_grad, jnp.transpose(weight_table, (2, 1, 0)), profile.reshape(1, T))])
    lo, lq, lk, lv, wq, wg, bnt, bnn, pul, k_near, v_near = parts
    block = min(T, 256)
    tile = pl.BlockSpec((block, H * D), lambda i: (i, 0))
    return pl.pallas_call(
        functools.partial(finish_kernel, (H, D, L, block)),
        grid=(T // block,),
        out_shape=[local] * 4,
        in_specs=[vm] * 11,
        out_specs=[tile] * 4,
        compiler_params=pltpu.CompilerParams(vmem_limit_bytes=24 * 1024 * 1024),
        name="finish",
    )(lo, lq, lk, lv, wq, wg, k_near, v_near, bnt, bnn, pul)


def solution(mesh):
    tokens = P(("col", "row"), None)
    return jax.shard_map(
        functools.partial(shards, mesh.shape["col"], mesh.shape["row"]),
        mesh=mesh,
        in_specs=(tokens,) * 4 + (P(), P(("col", "row"))),
        out_specs=(tokens,) * 4,
        check_vma=False,
    )
```

time: 28.3 us -> 23.6 us (0.83)
  Pallas kernels: 26 us -> 22.8 us
  local copies, waits for them, and re-layouts: 1.45 us -> 0 us
    pallas_call x1, Pallas kernels: 22.4 us -> 19.2 us  [shards(): pl.pallas_call(functools.partial(main_kernel, (T, H, D, cols, rows, span)...]
    unnamed x1 -> x0, local copies, waits for them, and re-layouts: 1.45 us -> none
where the time goes in v1:
time: 23.6 us; the launch traced here: 23.5 us
  Pallas kernels  22.8 us (97%)
  between operations  0.64 us (3%)
    pallas_call x1, Pallas kernels, shards(): pl.pallas_call(functools.partial(main_kernel, (T, H, D, cols, rows, span)...  19.2 us
    pallas_call x1, Pallas kernels, shards(): pl.pallas_call(functools.partial(finish_kernel, (H, D, L, block)), grid=(...  3.58 us

profile of v1, /device:TPU:0, one launch (start us, length us, event | category | flops | bytes accessed | tf_op | source)
XLA Modules:
  0.0 23.5 jit_solution(6904127572497388966)
XLA Ops:
  0.6 19.2 %main.1 = (f32[1024,256]{1,0:T(8,128)S(1)}, f32[1024,256]{1,0:T(8,128)S(1)}, f32[1024,256]{1,0:T(8,128)S(1)}, f32[1024,256]{1,0:T(8,128)S(1)}, bf16[1024,1280]{1...) custom-call(bf16[1024,256]{1,0:T(8,128)(2,1)} %q_hbm.1, ...), custom_call_target="tpu_custom_call" | custom-call | tf_op jit(solution)/shard_map/main/pallas_call | solution.py:383
  19.9 3.6 %finish.1 = (f32[1024,256]{1,0:T(8,128)}, f32[1024,256]{1,0:T(8,128)}, f32[1024,256]{1,0:T(8,128)}, f32[1024,256]{1,0:T(8,128)}) custom-call(f32[1024,256]{1,0:T(8,128)S(1)} %get-tuple-element.15.lo, f32[1024,256]{1,0:T(8,128)S(1)} %get-tuple-element.16.lq, f32[1024,256]{1,0:T(8,128)S(1)} %get-tuple-element.17.lk, f32[1024,256]{1,0:T(8,128)S(1)} %get-tuple-element.18.lv, ...), custom_call_target="tpu_custom_call" | custom-call | tf_op jit(solution)/shard_map/finish/pallas_call | solution.py:425

commit v2 on v1

--- a/solution.py
+++ b/solution.py
@@ -16,7 +16,20 @@
 TN = (((0,), (0,)), ((), ()))
 CHUNK = 128
 WIDE = 64
-CUTS = (1, 2, 3, 6)
+CUTS = (1, 2, 2, 6)
+SPAN = 256
+FLAT, DIRECT, POOLED = range(3)
+
+
+def level_kinds(L, D):
+    kinds = [None]
+    for j in range(1, L):
+        n = 1 << j - 1
+        kinds.append(FLAT if n <= 2 and j < L - 1 else DIRECT if n <= D // 16 else POOLED)
+    for j in range(1, L):
+        if any(kind != DIRECT for kind in kinds[j:]) and kinds[j] == DIRECT:
+            kinds[j] = POOLED
+    return kinds
 
 
 def mm(a, b, dims):
@@ -26,10 +39,10 @@
 def main_kernel(
     dims,
     q_hbm, k_hbm, v_hbm, g_hbm, tab_hbm, prof_hbm,
-    lo_ref, lq_ref, lk_ref, lv_ref, wq_ref, wg_ref, bnt_ref, bnn_ref, pul_ref, k_ref, v_ref,
+    lo_ref, lq_ref, lk_ref, lv_ref, wq_ref, wg_ref, bnt_ref, bnn_ref, pul_ref, bl_ref, k_ref, v_ref,
     q_ref, g_ref, tab_ref, prof_ref, in_sem,
-    tbl_scr, w_scr, lev_scr, m_scr, p_scr, d_scr,
-    s_scr, st, x0, pin, tots, far, ains, outs,
+    tbl_scr, w_scr, lev_scr, gt_scr, p_scr, d_scr,
+    s_scr, pl_scr, st, x0, pin, tots, far, ains, outs,
     pair_send, pair_recv, a_send, a_recv, b_send, b_recv, c_send, c_recv,
 ):
     T, H, D, cols, rows, span = dims
@@ -39,6 +52,9 @@
     top = L - 1
     tile_bits = T.bit_length() - 1
     span_bits = span.bit_length() - 1
+    blocks = T // span
+    LB = blocks.bit_length() - 1
+    K = L + LB
     z = lax.axis_index("col")
     row = lax.axis_index("row")
     core = lax.rem(row, 2)
@@ -111,8 +127,11 @@
             rs = slice(start, start + CHUNK)
             x = src[rs, h * D : (h + 1) * D].astype(F32)
             for j in js:
-                c = (h * L + j) * D
+                c = (h * K + j) * D
                 dst[rs, c : c + D] = (x * column(h, rs, tile_bits + 1 + j)).astype(BF16)
+
+    def weighed(h, low, high):
+        return wq_ref[:, (h * K + low) * D : (h * K + high) * D]
 
     def heads(h):
         return slice(h * D, (h + 1) * D)
@@ -121,13 +140,23 @@
     for h in range(H):
         weigh(q_ref, wq_ref, h, [top])
     loads[3].wait()
-    grads = [
-        mm(g_ref[:, heads(h)], wq_ref[:, (h * L + top) * D : (h * L + L) * D], TN) for h in range(H)
-    ]
+    for h in range(H):
+        gt_scr[h] = jnp.transpose(g_ref[:, heads(h)])
+    grads = [mm(gt_scr[h], weighed(h, top, L), NN) for h in range(H)]
     loads[4].wait()
     loads[5].wait()
     for h in range(H):
-        s_scr[h] = mm(v_ref[:, heads(h)], k_ref[:, heads(h)], TN)
+        parts = []
+        for i in range(blocks):
+            ts = slice(i * span, (i + 1) * span)
+            parts.append(mm(v_ref[ts, heads(h)], k_ref[ts, heads(h)], TN))
+        at = 0
+        for m in range(LB):
+            for group in range(0, len(parts), 2):
+                bl_ref[h, at] = parts[group].astype(BF16)
+                at += 1
+            parts = [parts[group] + parts[group + 1] for group in range(0, len(parts), 2)]
+        s_scr[h] = parts[0]
         st[top, h] = jnp.where(upper[top] == 1, grads[h], s_scr[h])
 
     def size(j):
@@ -137,21 +166,27 @@
     def piece(index, R):
         return pl.ds(pl.multiple_of(index * R, R), R)
 
-    direct = half <= D // 8
-
-    def start_direct():
-        n, owners, R = size(top)
-        mine = flipped(0, 0, top - 1)
+    kinds = level_kinds(L, D)
+
+    def start_direct(j):
+        n, owners, R = size(j)
+        mine = flipped(0, 0, j - 1)
         for flip in range(n - 1, -1, -1):
-            owner = flipped(flip, 0, top - 1)
+            owner = flipped(flip, 0, j - 1)
             for which in (core, other):
                 if flip == 0 and which is core:
                     continue
                 remote(
-                    st.at[top, which, piece(owner, R)], ains[top].at[mine * 2 + core],
-                    a_send.at[top], a_recv.at[top], device(flip, which),
+                    st.at[j, which, piece(owner, R)], ains[j].at[mine * 2 + core],
+                    a_send.at[j], a_recv.at[j], device(flip, which),
                 ).start()
-        ains[top][mine * 2 + core] = st[top, core, piece(mine, R), :]
+        ains[j][mine * 2 + core] = st[j, core, piece(mine, R), :]
+
+    def start_flat(j, source):
+        n = 1 << j - 1
+        slot = ains[j].at[flipped(0, 0, j - 1)] if n > 1 else far.at[j, core]
+        for flip in range(n, 2 * n):
+            remote(source, slot, b_send.at[j], b_recv.at[j], device(flip, core)).start()
 
     def start_reduce(j, source):
         n, owners, R = size(j)
@@ -198,8 +233,11 @@
             go()
 
     def arrived(j):
-        whole = far.at[j, core]
+        flat = kinds[j] == FLAT and j > 1
+        whole = ains[j] if flat else far.at[j, core]
         remote(whole, whole, b_send.at[j], b_recv.at[j], device(half, core)).wait_recv()
+        if flat:
+            far[j, core] = sum([ains[j][p] for p in range(1, 1 << j - 1)], ains[j][0])
 
     def settle(j):
         n, owners, R = size(j)
@@ -209,7 +247,9 @@
         def sent(ref, sem):
             remote(ref, ref, sem, a_recv.at[j], device(half, core)).wait_send()
 
-        if owners < n:
+        if kinds[j] == FLAT:
+            sent(ains[j], b_send.at[j])
+        elif owners < n:
             for flip in range(n - 1, 0, -1):
                 @pl.when(flipped(flip, 0, j - 1) < owners)
                 def _():
@@ -224,17 +264,25 @@
             sent(ains[j].at[pl.ds(0, n)], b_send.at[j])
 
     pl.semaphore_wait(barrier, len(greeted))
-    if direct:
-        start_direct()
-    for h in range(H):
-        weigh(q_ref, wq_ref, h, range(top))
-        low = mm(g_ref[:, heads(h)], wq_ref[:, h * L * D : (h * L + top) * D], TN)
+    if kinds[top] == DIRECT:
+        start_direct(top)
+    done = top
+    if kinds[top - 1] == DIRECT:
+        done = top - 1
+        for h in range(H):
+            weigh(q_ref, wq_ref, h, [done])
+            high = mm(gt_scr[h], weighed(h, done, top), NN)
+            st[done, h] = jnp.where(upper[done] == 1, high, s_scr[h])
+        start_direct(done)
+    for h in range(H):
+        weigh(q_ref, wq_ref, h, range(done))
+        low = mm(gt_scr[h], weighed(h, 0, done), NN)
         state = s_scr[h]
-        for j in range(1, top):
+        for j in range(1, done):
             st[j, h] = jnp.where(upper[j] == 1, low[:, j * D : (j + 1) * D], state)
         x0[h] = jnp.where(core == 0, state, low[:, :D])
     partner = device(0, other)
-    pooled = top if direct else L
+    pooled = min([j for j in range(1, L) if kinds[j] == DIRECT], default=L)
     pair = remote(
         st.at[pl.ds(1, pooled - 1), other], pin, pair_send.at[0], pair_recv.at[0], partner
     )
@@ -250,12 +298,36 @@
         lev = lev + jnp.where(apart >= 1 << bit, 1, 0)
     lev_scr[...] = jnp.where(c_at <= r_at, lev, -1)
 
-    last = T // span - 1
+    def local_states(h):
+        for i in range(1, blocks):
+            for start in range(i * span, (i + 1) * span, CHUNK):
+                rs = slice(start, start + CHUNK)
+                xq = q_ref[rs, heads(h)].astype(F32)
+                xg = g_ref[rs, heads(h)].astype(F32)
+                for m in range(LB):
+                    if i >> m & 1:
+                        c = (h * K + L + m) * D
+                        w = column(h, rs, span_bits + 1 + m)
+                        wq_ref[rs, c : c + D] = (xq * w).astype(BF16)
+                        wg_ref[rs, c : c + D] = (xg * w).astype(BF16)
+        pulls = [None] * blocks
+        for m in range(LB):
+            step = 1 << m
+            c = (h * K + L + m) * D
+            for low in range(0, blocks, 2 * step):
+                rs = slice((low + step) * span, (low + 2 * step) * span)
+                grad = mm(gt_scr[h, :, rs], wq_ref[rs, c : c + D], NN)
+                for i in range(low, low + step):
+                    pulls[i] = grad if pulls[i] is None else pulls[i] + grad
+        for i in range(blocks):
+            pl_scr[i, h] = jnp.zeros((D, D), F32) if pulls[i] is None else pulls[i]
 
     def unit(h, i):
         hs = heads(h)
         ts = slice(i * span, (i + 1) * span)
-        width = (i + 1) * span
+        q, k, v, g = q_ref[ts, hs], k_ref[ts, hs], v_ref[ts, hs], g_ref[ts, hs]
+        scores = mm(q, k, NT)
+        grad_scores = mm(g, v, NT)
         for start in range(0, span, 64):
             rs = slice(start, start + 64)
             wts = slice(i * span + start, i * span + start + 64)
@@ -263,30 +335,14 @@
             here = lev_scr[rs, :]
             for level in range(span_bits + 1):
                 mask = jnp.where(here == level, column(h, wts, level), mask)
-            m_scr[rs, :] = mask
-        q = q_ref[ts, hs]
-        g = g_ref[ts, hs]
-        for b in range(i + 1):
-            bs = slice(b * span, (b + 1) * span)
-            if b < i:
-                mask = column(h, ts, span_bits + (b ^ i).bit_length())
-            else:
-                mask = m_scr[...]
-            p_scr[:, bs] = (mm(q, k_ref[bs, hs], NT) * mask).astype(BF16)
-            d_scr[:, bs] = (mm(g, v_ref[bs, hs], NT) * mask).astype(BF16)
-        ws = slice(0, width)
-        lo_ref[ts, hs] = mm(p_scr[:, ws], v_ref[ws, hs], NN)
-        lq_ref[ts, hs] = mm(d_scr[:, ws], k_ref[ws, hs], NN)
-        dk = mm(d_scr[:, ws], q, TN)
-        dv = mm(p_scr[:, ws], g, TN)
-        if i == last:
-            lk_ref[ws, hs] = dk
-            lv_ref[ws, hs] = dv
-        else:
-            lk_ref[ws, hs] += dk
-            lv_ref[ws, hs] += dv
-
-    work = [(h, i) for i in range(last, -1, -1) for h in range(H)]
+            p_scr[rs, :] = (scores[rs, :] * mask).astype(BF16)
+            d_scr[rs, :] = (grad_scores[rs, :] * mask).astype(BF16)
+        lo_ref[ts, hs] = mm(p_scr[...], v, NN)
+        lq_ref[ts, hs] = mm(d_scr[...], k, NN)
+        lk_ref[ts, hs] = mm(d_scr[...], q, TN)
+        lv_ref[ts, hs] = mm(p_scr[...], g, TN)
+
+    work = [(h, i) for i in range(blocks) for h in range(H)]
 
     def units(start, end):
         for h, i in work[len(work) * start // 8 : len(work) * end // 8]:
@@ -296,32 +352,37 @@
     pair.wait()
     for j in range(pooled - 1, 0, -1):
         tots[j - 1] = st[j, core] + pin[j - 1]
-        if j == 1:
-            ains[1][0] = tots[0]
+        if kinds[j] == FLAT:
+            start_flat(j, tots.at[j - 1])
         else:
             start_reduce(j, tots.at[j - 1])
-    spread(1)
+    spreads = [j for j in range(top, 0, -1) if kinds[j] != FLAT]
     units(CUTS[0], CUTS[1])
-    spread(top)
+    spread(spreads[0])
     units(CUTS[1], CUTS[2])
-    for j in range(top - 1, 1, -1):
+    for j in spreads[1:]:
         spread(j)
     units(CUTS[2], CUTS[3])
-    for h in range(H):
-        weigh(g_ref, wg_ref, h, range(L))
-
     def relay(low, high, n):
         ref = far.at[pl.ds(low, high - low), core]
         copy = remote(ref, ref, c_send.at[n], c_recv.at[n], partner)
         copy.start()
         return copy
 
-    for j in range(1, top):
+    flats = [j for j in range(1, L) if kinds[j] == FLAT]
+    near.wait()
+    for j in flats:
         arrived(j)
-    early = relay(1, top, 0)
+    early = relay(1, 1 + len(flats), 0)
+    for h in range(H):
+        weigh(g_ref, wg_ref, h, range(L))
     units(CUTS[3], 8)
-    near.wait()
-    early.wait_recv()
+    for h in range(H):
+        local_states(h)
+    for j in range(1 + len(flats), top):
+        arrived(j)
+    middle = relay(1 + len(flats), top, 2)
+    early.wait()
 
     def gather(h, js, pulled):
         for j in js:
@@ -333,30 +394,59 @@
             bnn_ref[h, j * D : (j + 1) * D, :] = chosen
         return pulled
 
-    for h in range(H):
-        s_scr[h] = gather(h, range(top), jnp.zeros((D, D), F32))
+    split = 1 + len(flats)
+    for h in range(H):
+        s_scr[h] = gather(h, range(split), jnp.zeros((D, D), F32))
+    middle.wait()
+    for h in range(H):
+        s_scr[h] = gather(h, range(split, top), s_scr[h])
     arrived(top)
     late = relay(top, L, 1)
     for j in range(1, L):
         settle(j)
-    early.wait_send()
     late.wait()
     for h in range(H):
-        pul_ref[h] = gather(h, [top], s_scr[h]).astype(BF16)
+        pulled = gather(h, [top], s_scr[h])
+        for i in range(blocks):
+            pul_ref[i, h] = (pulled + pl_scr[i, h]).astype(BF16)
 
 
 def finish_kernel(
-    dims, lo, lq, lk, lv, wq, wg, k, v, bnt, bnn, pul, out, dq, dk, dv
+    dims, lo, lq, lk, lv, wq, wg, k, v, bnt, bnn, pul, bl,
+    out_hbm, dq_hbm, dk_hbm, dv_hbm, out, dq, dk, dv, sem,
 ):
-    H, D, L, block = dims
-    ts = pl.ds(pl.multiple_of(pl.program_id(0) * block, block), block)
-    for h in range(H):
-        hs = slice(h * D, (h + 1) * D)
-        ls = slice(h * L * D, (h + 1) * L * D)
-        out[:, hs] = lo[ts, hs] + mm(wq[ts, ls], bnt[h], NT)
-        dq[:, hs] = lq[ts, hs] + mm(wg[ts, ls], bnn[h], NN)
-        dk[:, hs] = lk[ts, hs] + mm(v[ts, hs], pul[h], NN)
-        dv[:, hs] = lv[ts, hs] + mm(k[ts, hs], pul[h], NT)
+    H, D, L, span = dims
+    blocks = lo.shape[0] // span
+    LB = blocks.bit_length() - 1
+    K = L + LB
+    copies = []
+    for i in range(blocks):
+        ts = slice(i * span, (i + 1) * span)
+        for h in range(H):
+            hs = slice(h * D, (h + 1) * D)
+            dk[ts, hs] = lk[ts, hs] + mm(v[ts, hs], pul[i, h], NN)
+            dv[ts, hs] = lv[ts, hs] + mm(k[ts, hs], pul[i, h], NT)
+            ls = slice(h * K * D, (h * K + L) * D)
+            o = lo[ts, hs] + mm(wq[ts, ls], bnt[h], NT)
+            b = lq[ts, hs] + mm(wg[ts, ls], bnn[h], NN)
+            at = 0
+            for m in range(LB):
+                if i >> m & 1:
+                    c = (h * K + L + m) * D
+                    state = bl[h, at + (i >> m + 1)]
+                    o = o + mm(wq[ts, c : c + D], state, NT)
+                    b = b + mm(wg[ts, c : c + D], state, NN)
+                at += blocks >> m + 1
+            out[ts, hs] = o
+            dq[ts, hs] = b
+        for n, (src, dst) in enumerate(
+            [(dk, dk_hbm), (dv, dv_hbm), (out, out_hbm), (dq, dq_hbm)]
+        ):
+            copy = pltpu.make_async_copy(src.at[ts], dst.at[ts], sem.at[i, n])
+            copy.start()
+            copies.append(copy)
+    for copy in copies:
+        copy.wait()
 
 
 def shards(cols, rows, queries, keys, values, out_grad, weight_table, profile):
@@ -367,28 +457,32 @@
     L = rows.bit_length() + cols.bit_length() - 2
     profiles = weight_table.shape[0]
     top = L - 1
-    direct = 1 << top - 1 <= D // 8
-    span = min(T, 256)
+    kinds = level_kinds(L, D)
+    pooled = min([j for j in range(1, L) if kinds[j] == DIRECT], default=L)
+    span = min(T, SPAN)
+    blocks = T // span
+    LB = blocks.bit_length() - 1
     assert H == 2 and L > 2 and H * WIDE == 128 and levels <= WIDE
-    pieces = [(8, D), (1, D, D)]
-    for j in range(2, L):
+    pieces = [(8, D)]
+    for j in range(1, L):
         n = 1 << j - 1
-        R = D // min(n, D // 8)
-        pieces.append((n * (2 if direct and j == top else 1), R, D))
+        R = D if kinds[j] == FLAT else D // min(n, D // 8)
+        pieces.append((n * (2 if kinds[j] == DIRECT else 1), R, D))
     vm = pl.BlockSpec(memory_space=pltpu.VMEM)
     sds = jax.ShapeDtypeStruct
     dma = pltpu.SemaphoreType.DMA
     local = sds((T, H * D), F32)
-    weighted = sds((T, H * L * D), BF16)
+    weighted = sds((T, H * (L + LB) * D), BF16)
     parts = pl.pallas_call(
         functools.partial(main_kernel, (T, H, D, cols, rows, span)),
         out_shape=[
             local, local, local, local, weighted, weighted,
-            sds((H, D, L * D), BF16), sds((H, L * D, D), BF16), sds((H, D, D), BF16),
+            sds((H, D, L * D), BF16), sds((H, L * D, D), BF16), sds((blocks, H, D, D), BF16),
+            sds((H, max(blocks - 1, 1), D, D), BF16),
             sds((T, H * D), BF16), sds((T, H * D), BF16),
         ],
         in_specs=[pl.BlockSpec(memory_space=pltpu.HBM)] * 6,
-        out_specs=[vm] * 11,
+        out_specs=[vm] * 12,
         scratch_shapes=[
             pltpu.VMEM((T, H * D), BF16),
             pltpu.VMEM((T, H * D), BF16),
@@ -398,39 +492,38 @@
             pltpu.VMEM((profiles, H * WIDE), F32),
             pltpu.VMEM((T, H * WIDE), F32),
             pltpu.VMEM((span, span), jnp.int32),
-            pltpu.VMEM((span, span), F32),
-            pltpu.VMEM((span, T), BF16),
-            pltpu.VMEM((span, T), BF16),
+            pltpu.VMEM((H, D, T), BF16),
+            pltpu.VMEM((span, span), BF16),
+            pltpu.VMEM((span, span), BF16),
             pltpu.VMEM((H, D, D), F32),
+            pltpu.VMEM((blocks, H, D, D), F32),
             pltpu.VMEM((L, H, D, D), F32),
             pltpu.VMEM((H, D, D), F32),
-            pltpu.VMEM(((top if direct else L) - 1, D, D), F32),
-            pltpu.VMEM(((top if direct else L) - 1, D, D), F32),
+            pltpu.VMEM((pooled - 1, D, D), F32),
+            pltpu.VMEM((pooled - 1, D, D), F32),
             pltpu.VMEM((L, H, D, D), F32),
             [pltpu.VMEM(shape, F32) for shape in pieces],
             [pltpu.VMEM(shape[-2:], F32) for shape in pieces],
             dma((2,)), dma((2,)),
             dma((L,)), dma((L,)),
             dma((L,)), dma((L,)),
-            dma((2,)), dma((2,)),
+            dma((3,)), dma((3,)),
         ],
         compiler_params=pltpu.CompilerParams(
             collective_id=0, has_side_effects=True, vmem_limit_bytes=40 * 1024 * 1024
         ),
         name="main",
     )(*[pltpu.with_memory_space_constraint(a, pltpu.HBM) for a in (queries, keys, values, out_grad, jnp.transpose(weight_table, (2, 1, 0)), profile.reshape(1, T))])
-    lo, lq, lk, lv, wq, wg, bnt, bnn, pul, k_near, v_near = parts
-    block = min(T, 256)
-    tile = pl.BlockSpec((block, H * D), lambda i: (i, 0))
+    lo, lq, lk, lv, wq, wg, bnt, bnn, pul, bl, k_near, v_near = parts
     return pl.pallas_call(
-        functools.partial(finish_kernel, (H, D, L, block)),
-        grid=(T // block,),
+        functools.partial(finish_kernel, (H, D, L, span)),
         out_shape=[local] * 4,
-        in_specs=[vm] * 11,
-        out_specs=[tile] * 4,
+        in_specs=[vm] * 12,
+        out_specs=[pl.BlockSpec(memory_space=pltpu.HBM)] * 4,
+        scratch_shapes=[pltpu.VMEM((T, H * D), F32)] * 4 + [dma((blocks, 4))],
         compiler_params=pltpu.CompilerParams(vmem_limit_bytes=24 * 1024 * 1024),
         name="finish",
-    )(lo, lq, lk, lv, wq, wg, k_near, v_near, bnt, bnn, pul)
+    )(lo, lq, lk, lv, wq, wg, k_near, v_near, bnt, bnn, pul, bl)
 
 
 def solution(mesh):

time: 23.6 us -> 21.9 us (0.928)
  Pallas kernels: 22.8 us -> 21.1 us
    pallas_call x1, Pallas kernels: 19.2 us -> 18.1 us  [shards(): pl.pallas_call(functools.partial(main_kernel, (T, H, D, cols, rows, span)...]
    pallas_call x1, Pallas kernels: 3.58 us -> 2.97 us  [shards(): pl.pallas_call(functools.partial(finish_kernel, (H, D, L, span)), out_sha...]
where the time goes in v2:
time: 21.9 us; the launch traced here: 21.7 us
  Pallas kernels  21.1 us (96%)
  between operations  0.64 us (3%)
    pallas_call x1, Pallas kernels, shards(): pl.pallas_call(functools.partial(main_kernel, (T, H, D, cols, rows, span)...  18.1 us
    pallas_call x1, Pallas kernels, shards(): pl.pallas_call(functools.partial(finish_kernel, (H, D, L, span)), out_sha...  2.97 us

profile of v2, /device:TPU:0, one launch (start us, length us, event | category | flops | bytes accessed | tf_op | source)
XLA Modules:
  0.0 21.7 jit_solution(8853125760815076613)
XLA Ops:
  0.6 18.1 %main.1 = (f32[1024,256]{1,0:T(8,128)S(1)}, f32[1024,256]{1,0:T(8,128)S(1)}, f32[1024,256]{1,0:T(8,128)S(1)}, f32[1024,256]{1,0:T(8,128)S(1)}, bf16[1024,1792]{1...) custom-call(bf16[1024,256]{1,0:T(8,128)(2,1)} %q_hbm.1, ...), custom_call_target="tpu_custom_call" | custom-call | tf_op jit(solution)/shard_map/main/pallas_call | solution.py:476
  18.8 3.0 %finish.1 = (f32[1024,256]{1,0:T(8,128)}, f32[1024,256]{1,0:T(8,128)}, f32[1024,256]{1,0:T(8,128)}, f32[1024,256]{1,0:T(8,128)}) custom-call(f32[1024,256]{1,0:T(8,128)S(1)} %get-tuple-element.16.lo, f32[1024,256]{1,0:T(8,128)S(1)} %get-tuple-element.17.lq, f32[1024,256]{1,0:T(8,128)S(1)} %get-tuple-element.18.lk, f32[1024,256]{1,0:T(8,128)S(1)} %get-tuple-element.19.lv, ...), custom_call_target="tpu_custom_call" | custom-call | tf_op jit(solution)/shard_map/finish/pallas_call | solution.py:518

commit v3 on v2

--- a/solution.py
+++ b/solution.py
@@ -16,7 +16,7 @@
 TN = (((0,), (0,)), ((), ()))
 CHUNK = 128
 WIDE = 64
-CUTS = (1, 2, 2, 6)
+CUTS = (1, 2, 3, 7)
 SPAN = 256
 FLAT, DIRECT, POOLED = range(3)
 
@@ -379,9 +379,9 @@
     units(CUTS[3], 8)
     for h in range(H):
         local_states(h)
-    for j in range(1 + len(flats), top):
+    for j in range(1 + len(flats), L):
         arrived(j)
-    middle = relay(1 + len(flats), top, 2)
+    late = relay(1 + len(flats), L, 1)
     early.wait()
 
     def gather(h, js, pulled):
@@ -397,16 +397,11 @@
     split = 1 + len(flats)
     for h in range(H):
         s_scr[h] = gather(h, range(split), jnp.zeros((D, D), F32))
-    middle.wait()
-    for h in range(H):
-        s_scr[h] = gather(h, range(split, top), s_scr[h])
-    arrived(top)
-    late = relay(top, L, 1)
     for j in range(1, L):
         settle(j)
     late.wait()
     for h in range(H):
-        pulled = gather(h, [top], s_scr[h])
+        pulled = gather(h, range(split, L), s_scr[h])
         for i in range(blocks):
             pul_ref[i, h] = (pulled + pl_scr[i, h]).astype(BF16)
 
@@ -507,7 +502,7 @@
             dma((2,)), dma((2,)),
             dma((L,)), dma((L,)),
             dma((L,)), dma((L,)),
-            dma((3,)), dma((3,)),
+            dma((2,)), dma((2,)),
         ],
         compiler_params=pltpu.CompilerParams(
             collective_id=0, has_side_effects=True, vmem_limit_bytes=40 * 1024 * 1024

time: 21.9 us -> 21 us (0.959)
  Pallas kernels: 21.1 us -> 20.2 us
    pallas_call x1, Pallas kernels: 18.1 us -> 17.2 us  [shards(): pl.pallas_call(functools.partial(main_kernel, (T, H, D, cols, rows, span)...]
where the time goes in v3:
time: 21 us; the launch traced here: 20.8 us
  Pallas kernels  20.2 us (96%)
  between operations  0.64 us (3%)
    pallas_call x1, Pallas kernels, shards(): pl.pallas_call(functools.partial(main_kernel, (T, H, D, cols, rows, span)...  17.2 us
    pallas_call x1, Pallas kernels, shards(): pl.pallas_call(functools.partial(finish_kernel, (H, D, L, span)), out_sha...  2.97 us

profile of v3, /device:TPU:0, one launch (start us, length us, event | category | flops | bytes accessed | tf_op | source)
XLA Modules:
  0.0 20.8 jit_solution(7574918005264864665)
XLA Ops:
  0.6 17.2 %main.1 = (f32[1024,256]{1,0:T(8,128)S(1)}, f32[1024,256]{1,0:T(8,128)S(1)}, f32[1024,256]{1,0:T(8,128)S(1)}, f32[1024,256]{1,0:T(8,128)S(1)}, bf16[1024,1792]{1...) custom-call(bf16[1024,256]{1,0:T(8,128)(2,1)} %q_hbm.1, ...), custom_call_target="tpu_custom_call" | custom-call | tf_op jit(solution)/shard_map/main/pallas_call | solution.py:471
  17.9 3.0 %finish.1 = (f32[1024,256]{1,0:T(8,128)}, f32[1024,256]{1,0:T(8,128)}, f32[1024,256]{1,0:T(8,128)}, f32[1024,256]{1,0:T(8,128)}) custom-call(f32[1024,256]{1,0:T(8,128)S(1)} %get-tuple-element.16.lo, f32[1024,256]{1,0:T(8,128)S(1)} %get-tuple-element.17.lq, f32[1024,256]{1,0:T(8,128)S(1)} %get-tuple-element.18.lk, f32[1024,256]{1,0:T(8,128)S(1)} %get-tuple-element.19.lv, ...), custom_call_target="tpu_custom_call" | custom-call | tf_op jit(solution)/shard_map/finish/pallas_call | solution.py:513
